TPU v7x, 32 devices: a whole 2x2x4 slice. The times are simulated.
32 devices in a mesh: seq: 8 (over z, y), samp: 4 (over x, core).
Axes of the slice: x: 2, y: 2, z: 4, core: 2. Of those that a mesh axis runs over, the one named last changes fastest.
Arguments:
- queries: bfloat16 [4, 1024, 5120], P('samp', 'seq'), may hold values from -120 to 120
- prefix_keys: bfloat16 [1024, 1024], P('seq'), may hold values from -4 to 4
- prefix_values: bfloat16 [1024, 1024], P('seq'), may hold values from -4 to 4
- suffix_keys: bfloat16 [4, 1024, 1024], P('samp', 'seq'), may hold values from -5 to 5
- suffix_values: bfloat16 [4, 1024, 1024], P('samp', 'seq'), may hold values from -4 to 4
- layout_pre: int32 [4, 8, 8], P('samp', 'seq'), may hold values 0 or 1
- layout_suf: int32 [4, 8, 8], P('samp', 'seq'), may hold values 0 or 1
- lengths: int32 [4], P('samp'), may hold values from 1 to 8
Outputs:
- attended: bfloat16 [4, 1024, 5120], P('samp', 'seq')
All inputs are finite; a program needn't handle non-finite values. No bound on the sum of `layout_pre` or of `layout_suf` on one device may be relied on, other than what follows from the above.
Results may differ from a plain program's by a relative error of at most 0.004.
Values may be sent and summed in bfloat16 or wider, within the bound.
No kernel may reach another device: no remote copies, remote signals or barrier semaphores. Data moves between devices by JAX's collectives and lax.ppermute only.
A program may use at most 128 MiB of HBM per device.

v0:
```python
import math
import jax
import jax.numpy as jnp
from jax import lax
from jax.sharding import PartitionSpec as P

HEADS = 40
KV_HEADS = 8
HEAD_DIM = 128
BLOCK = 128
masked_value = -1e30


def block_size(count):
    return math.gcd(count, 512)


def softmax_step(carry, scores, allowed, value_rows, form):
    run_max, run_sum, run_total = carry
    key_mask = allowed[:, None, None, :, :]
    block_max = jnp.max(jnp.where(key_mask, scores, masked_value), axis=-1)
    new_max = jnp.maximum(run_max, block_max)
    weights = jnp.where(key_mask, jnp.exp(scores - new_max[..., None]), 0.0)
    scale_old = jnp.exp(run_max - new_max)
    new_sum = run_sum * scale_old + jnp.sum(weights, axis=-1)
    rounded = weights.astype(jnp.bfloat16)
    added = jnp.einsum(form, rounded, value_rows, preferred_element_type=jnp.float32)
    rescale = jnp.transpose(scale_old, (0, 3, 1, 2))[..., None]
    return (new_max, new_sum, run_total * rescale + added)


def lookup(table, block_ids):
    columns = jnp.arange(table.shape[1], dtype=jnp.int32)
    onehot = (block_ids[None, :] == columns[:, None]).astype(jnp.int32)
    return jnp.sum(table[:, :, None] * onehot[None, :, :], axis=1) > 0


def shards(
    queries, prefix_keys, prefix_values, suffix_keys, suffix_values, layout_pre, layout_suf, lengths
):
    group_size = HEADS // KV_HEADS
    score_scale = 1.0 / math.sqrt(HEAD_DIM)
    samples = queries.shape[0]
    query_block = lax.axis_index("seq")
    query_grid = queries.reshape(samples, BLOCK, KV_HEADS, group_size, HEAD_DIM)
    query_position = query_block * BLOCK + jnp.arange(BLOCK, dtype=jnp.int32)
    pre_table = layout_pre[:, 0, :]
    suf_table = layout_suf[:, 0, :]
    start_carry = (
        jnp.full((samples, KV_HEADS, group_size, BLOCK), masked_value, jnp.float32),
        jnp.zeros((samples, KV_HEADS, group_size, BLOCK), jnp.float32),
        jnp.zeros((samples, BLOCK, KV_HEADS, group_size, HEAD_DIM), jnp.float32),
    )
    share = prefix_keys.shape[0] // lax.axis_size("samp")
    seq_count = lax.axis_size("seq")
    shard_rows = prefix_keys.shape[0]
    share_start = lax.axis_index("samp") * share
    own_keys = lax.dynamic_slice_in_dim(prefix_keys, share_start, share, 0)
    own_values = lax.dynamic_slice_in_dim(prefix_values, share_start, share, 0)
    shares = (
        lax.all_gather(own_keys, "seq", axis=0, tiled=True),
        lax.all_gather(own_values, "seq", axis=0, tiled=True),
    )
    pieces = (
        lax.all_gather(shares[0], "samp", axis=0, tiled=True),
        lax.all_gather(shares[1], "samp", axis=0, tiled=True),
    )
    whole_index = jnp.arange(pieces[0].shape[0], dtype=jnp.int32)
    owner_share = whole_index // (seq_count * share)
    remainder = whole_index % (seq_count * share)
    positions = remainder // share * shard_rows + owner_share * share + remainder % share
    carry = start_carry
    key_rows = pieces[0]
    value_rows = pieces[1]
    count = key_rows.shape[0]
    prefix_size = block_size(count)
    steps = count // prefix_size

    def prefix_one_step(inner, pieces):
        key_part, value_part, place = pieces
        key_grid = key_part.reshape(prefix_size, KV_HEADS, HEAD_DIM)
        value_grid = value_part.reshape(prefix_size, KV_HEADS, HEAD_DIM)
        scores = (
            jnp.einsum("sqgjd,rgd->sgjqr", query_grid, key_grid, preferred_element_type=jnp.float32)
            * score_scale
        )
        seen = lookup(pre_table, place // BLOCK)
        allowed = jnp.broadcast_to(seen[:, None, :], (samples, BLOCK, prefix_size))
        return (softmax_step(inner, scores, allowed, value_grid, "sgjqr,rgd->sqgjd"), None)

    width = key_rows.shape[1]
    carry, unused = lax.scan(
        prefix_one_step,
        carry,
        (
            key_rows.reshape(steps, prefix_size, width),
            value_rows.reshape(steps, prefix_size, width),
            positions.reshape(steps, prefix_size),
        ),
    )
    suffix_carry = carry
    key_rows = lax.all_gather(suffix_keys, "seq", axis=1, tiled=True)
    value_rows = lax.all_gather(suffix_values, "seq", axis=1, tiled=True)
    count = key_rows.shape[1]
    size = block_size(count)
    steps = count // size
    width = key_rows.shape[2]
    positions = jnp.arange(count, dtype=jnp.int32).reshape(steps, size)

    def suffix_one_step(inner, items):
        key_part, value_part, place = items
        key_grid = key_part.reshape(samples, size, KV_HEADS, HEAD_DIM)
        value_grid = value_part.reshape(samples, size, KV_HEADS, HEAD_DIM)
        scores = (
            jnp.einsum(
                "sqgjd,srgd->sgjqr", query_grid, key_grid, preferred_element_type=jnp.float32
            )
            * score_scale
        )
        key_block = place // BLOCK
        block_seen = (key_block == query_block)[None, :] | lookup(suf_table, key_block)
        causal = place[None, :] <= query_position[:, None]
        allowed = block_seen[:, None, :] & causal[None, :, :]
        return (softmax_step(inner, scores, allowed, value_grid, "sgjqr,srgd->sqgjd"), None)

    key_steps = jnp.transpose(key_rows.reshape(samples, steps, size, width), (1, 0, 2, 3))
    value_steps = jnp.transpose(value_rows.reshape(samples, steps, size, width), (1, 0, 2, 3))
    suffix_carry, unused = lax.scan(
        suffix_one_step, suffix_carry, (key_steps, value_steps, positions)
    )
    carry = suffix_carry
    run_max, run_sum, run_total = carry
    mixed = run_total / jnp.transpose(run_sum, (0, 3, 1, 2))[..., None]
    mixed = mixed.reshape(samples, BLOCK, HEADS * HEAD_DIM)
    is_live = (query_block < lengths)[:, None, None]
    return jnp.where(is_live, mixed, 0.0).astype(jnp.bfloat16)


def solution(mesh):
    return jax.shard_map(
        shards,
        mesh=mesh,
        in_specs=(
            P("samp", "seq", None),
            P("seq", None),
            P("seq", None),
            P("samp", "seq", None),
            P("samp", "seq", None),
            P("samp", "seq", None),
            P("samp", "seq", None),
            P("samp"),
        ),
        out_specs=P("samp", "seq", None),
        check_vma=False,
    )
```

profile of v0, /device:TPU:0, one launch (start us, length us, event | category | flops | bytes accessed | tf_op | source)
XLA Modules:
  0.0 262.5 jit_solution(15586592918994311306)
XLA Ops:
  6.5 0.9 copy-done
  7.5 35.3 %all_gather.18 = bf16[256,1024]{1,0:T(8,128)(2,1)} all-gather(bf16[32,1024]{1,0:T(8,128)(2,1)S(1)} %constant_dynamic-slice_fusion.6), channel_id=1, replica_groups=mesh['seq'=8,'samp'=4] {'seq'}, dimensions={0}, use_global_device_ids=true | all-gather | bytes 589824 | tf_op jit(solution)/shard_map/all_gather | solution.py:61
  42.8 0.9 constant_dynamic-slice_fusion.5
  43.7 33.2 %all_gather.20 = bf16[256,1024]{1,0:T(8,128)(2,1)} all-gather(bf16[32,1024]{1,0:T(8,128)(2,1)S(1)} %constant_dynamic-slice_fusion.5), channel_id=1, replica_groups=mesh['seq'=8,'samp'=4] {'seq'}, dimensions={0}, use_global_device_ids=true | all-gather | bytes 589824 | tf_op jit(solution)/shard_map/all_gather | solution.py:62
  76.9 0.7 all-gather.9.cloned.1.call-update
  77.7 0.5 all-gather.11.cloned.1.call-update
  78.3 0.8 copy.38
  79.1 1.4 copy.40
  81.2 19.7 %all-gather.7.cloned.1.call-done = bf16[1024,1024]{1,0:T(8,128)(2,1)} async-done(((bf16[256,1024]{1,0:T(8,128)(2,1)}), bf16[1024,1024]{1,0:T(8,128)(2,1)}) %all-gather.7.cloned.1.call-update) | async-done | bytes 2097168 | tf_op jit(solution)/shard_map/all_gather | solution.py:66
  100.9 45.4 %while.35 = (s32[]{:T(128)}, f32[1,8,5,128]{3,2,1,0:T(8,128)S(1)}, f32[1,8,5,128]{3,2,1,0:T(8,128)}, f32[1,128,8,5,128]{1,4,3,2,0:T(8,128)}, s32[2,512]{1,0:T(2,...) while((s32[]{:T(128)}, f32[1,8,5,128]{3,2,1,0:T(8,128)S(1)}, ...), condition=%wide.region_4.5_spmd.clone, body=%wide.region_0.4_spmd.clone.sunk | while | flops 1373029888 | bytes 80294112 | solution.py:92
  101.0 1.7 constant_dynamic-slice_fusion.11
  102.7 0.5 copy.66
  103.3 6.7 %fusion.66 = (f32[8,5,128]{2,1,0:T(8,128)S(1)}, f32[8,512,128,5]{2,1,3,0:T(8,128)}) fusion(pred[512]{0:T(512)(128)(4,1)S(1)} %broadcast_compare_fusion.5, bf16[512,8,128,1]{0,2,3,1:T(8,128)(2,1)S(1)} %bitcast.194, bf16[1,128,8,5,128]{4,1,3,2,0:T(8,128)(2,1)} %get-tuple-element.613), kind=kOutput, calls=%fused_computation.3.clone.1 | convolution fusion | flops 678947840 | bytes 12866048 | tf_op jit(solution)/shard_map/while/body/eval_jaxpr/sqgjd,rgd->sgjqr/dot_general | solution.py:84
  110.0 1.4 copy.67
  111.4 8.5 %bitcast_add_fusion.11 = f32[1,128,8,5,128]{1,4,3,2,0:T(8,128)} fusion(f32[1,128,8,5,128]{1,4,3,2,0:T(8,128)} %get-tuple-element.598, bf16[512,8,128,1]{0,2,3,1:T(8,128)(2,1)} %bitcast.197, f32[8,512,128,5]{2,1,3,0:T(8,128)} %get-tuple-element.581, f32[8,5,128]{2,1,0:T(8,128)S(1)} %bitcast.200, pred[512]{0:T(512)(128)(4,1)S(1)} %broadcast_compare_fusion.5, ...), kind=kOutput, calls=%fused_computation.14.clone.1 | convolution fusion | flops 683540480 | bytes 16818688 | tf_op jit(solution)/shard_map/while/body/eval_jaxpr/sgjqr,rgd->sqgjd/dot_general | solution.py:27
  119.8 2.3 fusion.68
  122.1 0.6 bitcast_add_fusion.10
  122.9 1.7 constant_dynamic-slice_fusion.11
  124.6 0.5 copy.66
  125.2 6.8 %fusion.66 = (f32[8,5,128]{2,1,0:T(8,128)S(1)}, f32[8,512,128,5]{2,1,3,0:T(8,128)}) fusion(pred[512]{0:T(512)(128)(4,1)S(1)} %broadcast_compare_fusion.5, bf16[512,8,128,1]{0,2,3,1:T(8,128)(2,1)S(1)} %bitcast.194, bf16[1,128,8,5,128]{4,1,3,2,0:T(8,128)(2,1)} %get-tuple-element.613), kind=kOutput, calls=%fused_computation.3.clone.1 | convolution fusion | flops 678947840 | bytes 12866048 | tf_op jit(solution)/shard_map/while/body/eval_jaxpr/sqgjd,rgd->sgjqr/dot_general | solution.py:84
  132.0 1.4 copy.67
  133.3 9.2 %bitcast_add_fusion.11 = f32[1,128,8,5,128]{1,4,3,2,0:T(8,128)} fusion(f32[1,128,8,5,128]{1,4,3,2,0:T(8,128)} %get-tuple-element.598, bf16[512,8,128,1]{0,2,3,1:T(8,128)(2,1)} %bitcast.197, f32[8,512,128,5]{2,1,3,0:T(8,128)} %get-tuple-element.581, f32[8,5,128]{2,1,0:T(8,128)S(1)} %bitcast.200, pred[512]{0:T(512)(128)(4,1)S(1)} %broadcast_compare_fusion.5, ...), kind=kOutput, calls=%fused_computation.14.clone.1 | convolution fusion | flops 683540480 | bytes 16818688 | tf_op jit(solution)/shard_map/while/body/eval_jaxpr/sgjqr,rgd->sqgjd/dot_general | solution.py:27
  142.6 2.3 fusion.68
  144.9 1.4 bitcast_add_fusion.10
  146.3 5.9 %all-gather.9.cloned.1.call-done = bf16[1,1024,1024]{2,1,0:T(8,128)(2,1)} async-done(((bf16[1,128,1024]{2,1,0:T(8,128)(2,1)}), bf16[1,1024,1024]{2,1,0:T(8,128)(2,1)}) %all-gather.9.cloned.1.call-update) | async-done | bytes 2097168 | tf_op jit(solution)/shard_map/all_gather | solution.py:102
  152.2 49.6 %all-gather.11.cloned.1.call-done = bf16[1,1024,1024]{2,1,0:T(8,128)(2,1)} async-done(((bf16[1,128,1024]{2,1,0:T(8,128)(2,1)}), bf16[1,1024,1024]{2,1,0:T(8,128)(2,1)}) %all-gather.11.cloned.1.call-update) | async-done | bytes 2097168 | tf_op jit(solution)/shard_map/all_gather | solution.py:103
  201.8 50.6 %while.34 = (s32[]{:T(128)}, f32[1,8,5,128]{3,2,1,0:T(8,128)S(1)}, f32[1,8,5,128]{3,2,1,0:T(8,128)}, f32[1,128,8,5,128]{1,4,3,2,0:T(8,128)}, s32[2,512]{1,0:T(2,...) while((s32[]{:T(128)}, f32[1,8,5,128]{3,2,1,0:T(8,128)S(1)}, ...), condition=%wide.region_9.10_spmd.clone, body=%wide.region_5.9_spmd.clone.sunk | while | flops 1372491392 | bytes 80563432 | solution.py:128
  201.8 0.7 select_reduce_fusion.4
  202.6 0.2 compare_and_fusion.2
  202.8 1.7 constant_dynamic-slice_fusion.10
  204.5 0.5 copy.64
  205.1 7.2 %fusion.60 = (f32[8,5,128]{2,1,0:T(8,128)S(1)}, f32[8,512,128,5]{2,1,3,0:T(8,128)}) fusion(pred[128,512]{0,1:T(8,128)(4,1)S(1)} %compare_and_fusion.2, bf16[512,8,128,1]{0,2,3,1:T(8,128)(2,1)S(1)} %bitcast.195, bf16[1,128,8,5,128]{4,1,3,2,0:T(8,128)(2,1)} %get-tuple-element.649), kind=kOutput, calls=%fused_computation.36.clone.1 | convolution fusion | flops 678947840 | bytes 12931072 | tf_op jit(solution)/shard_map/while/body/eval_jaxpr/sqgjd,srgd->sgjqr/dot_general | solution.py:115
  212.3 0.6 fusion.61
  212.9 1.4 copy.65
  214.3 9.1 %bitcast_add_fusion.9 = f32[1,128,8,5,128]{1,4,3,2,0:T(8,128)} fusion(f32[1,128,8,5,128]{1,4,3,2,0:T(8,128)} %get-tuple-element.632, bf16[512,8,128,1]{0,2,3,1:T(8,128)(2,1)} %bitcast.196, f32[8,512,128,5]{2,1,3,0:T(8,128)} %get-tuple-element.566, f32[8,5,128]{2,1,0:T(8,128)S(1)} %bitcast.198, pred[128,512]{0,1:T(8,128)(4,1)S(1)} %compare_and_fusion.2, ...), kind=kOutput, calls=%fused_computation.47.clone.1 | convolution fusion | flops 682885120 | bytes 16883712 | tf_op jit(solution)/shard_map/while/body/eval_jaxpr/sgjqr,srgd->sqgjd/dot_general | solution.py:27
  223.5 2.3 fusion.62
  225.7 1.4 bitcast_add_fusion.8
  227.1 0.7 select_reduce_fusion.4
  228.1 1.7 constant_dynamic-slice_fusion.10
  229.9 0.5 copy.64
  230.4 7.2 %fusion.60 = (f32[8,5,128]{2,1,0:T(8,128)S(1)}, f32[8,512,128,5]{2,1,3,0:T(8,128)}) fusion(pred[128,512]{0,1:T(8,128)(4,1)S(1)} %compare_and_fusion.2, bf16[512,8,128,1]{0,2,3,1:T(8,128)(2,1)S(1)} %bitcast.195, bf16[1,128,8,5,128]{4,1,3,2,0:T(8,128)(2,1)} %get-tuple-element.649), kind=kOutput, calls=%fused_computation.36.clone.1 | convolution fusion | flops 678947840 | bytes 12931072 | tf_op jit(solution)/shard_map/while/body/eval_jaxpr/sqgjd,srgd->sgjqr/dot_general | solution.py:115
  237.6 0.6 fusion.61
  238.3 1.4 copy.65
  239.6 9.1 %bitcast_add_fusion.9 = f32[1,128,8,5,128]{1,4,3,2,0:T(8,128)} fusion(f32[1,128,8,5,128]{1,4,3,2,0:T(8,128)} %get-tuple-element.632, bf16[512,8,128,1]{0,2,3,1:T(8,128)(2,1)} %bitcast.196, f32[8,512,128,5]{2,1,3,0:T(8,128)} %get-tuple-element.566, f32[8,5,128]{2,1,0:T(8,128)S(1)} %bitcast.198, pred[128,512]{0,1:T(8,128)(4,1)S(1)} %compare_and_fusion.2, ...), kind=kOutput, calls=%fused_computation.47.clone.1 | convolution fusion | flops 682885120 | bytes 16883712 | tf_op jit(solution)/shard_map/while/body/eval_jaxpr/sgjqr,srgd->sqgjd/dot_general | solution.py:27
  248.8 2.3 fusion.62
  251.0 1.4 bitcast_add_fusion.8
  252.4 2.1 select_convert_fusion
  254.6 1.4 copy.45
  (67 shorter events, 0.9 us)
Async XLA Ops:
  6.5 1.0 copy-start
  6.5 71.8 %copy-start.1 = (bf16[1,128,5120]{2,1,0:T(8,128)(2,1)S(1)}, bf16[1,128,5120]{2,1,0:T(8,128)(2,1)}, u32[]{:S(2)}) copy-start(bf16[1,128,5120]{2,1,0:T(8,128)(2,1)} %param.12) | copy-start | bytes 3932164
  6.5 74.7 %all-gather.5.cloned.1.call-start = ((), (), s32[]{:S(2)}) async-start(), calls=%async_computation | async-start | bytes 2621440 | tf_op jit(solution)/shard_map/all_gather | solution.py:65
  42.8 58.1 %all-gather.7.cloned.1.call-start = ((), (), s32[]{:S(2)}) async-start(), calls=%async_computation.1 | async-start | bytes 2621440 | tf_op jit(solution)/shard_map/all_gather | solution.py:66
  76.9 75.3 %all-gather.9.cloned.1.call-start = ((), (), s32[]{:S(2)}) async-start(), calls=%async_computation.2 | async-start | bytes 2359296 | tf_op jit(solution)/shard_map/all_gather | solution.py:102
  77.6 124.2 %all-gather.11.cloned.1.call-start = ((), (), s32[]{:S(2)}) async-start(), calls=%async_computation.3 | async-start | bytes 2359296 | tf_op jit(solution)/shard_map/all_gather | solution.py:103
  78.3 22.6 %copy-start.2 = (s32[1,1,8]{2,1,0:T(1,128)S(1)}, s32[1,1,8]{2,1,0:T(1,128)}, u32[]{:S(2)}) copy-start(s32[1,1,8]{2,1,0:T(1,128)} %param.17) | copy-start | bytes 100
  110.0 9.8 %slice-start.3 = ((s8[10485760]{0:T(1024)(128)(4,1)}), s8[2097152]{0:T(1024)(128)(4,1)S(1)}, s32[]{:S(2)}) async-start(s8[10485760]{0:T(1024)(128)(4,1)} %bitcast.192), calls=%async_computation.7 | async-start | bytes 4194304 | tf_op jit(solution)/shard_map/while
  111.4 8.5 %slice-start.4 = ((s8[10485760]{0:T(1024)(128)(4,1)}), s8[4194304]{0:T(1024)(128)(4,1)S(1)}, s32[]{:S(2)}) async-start(s8[10485760]{0:T(1024)(128)(4,1)} %bitcast.192), calls=%async_computation.8 | async-start | bytes 8388608 | tf_op jit(solution)/shard_map/while
  111.4 8.5 %slice-start.5 = ((s8[10485760]{0:T(1024)(128)(4,1)}), s8[4194304]{0:T(1024)(128)(4,1)S(1)}, s32[]{:S(2)}) async-start(s8[10485760]{0:T(1024)(128)(4,1)} %bitcast.192), calls=%async_computation.9 | async-start | bytes 8388608 | tf_op jit(solution)/shard_map/while
  132.0 10.6 %slice-start.3 = ((s8[10485760]{0:T(1024)(128)(4,1)}), s8[2097152]{0:T(1024)(128)(4,1)S(1)}, s32[]{:S(2)}) async-start(s8[10485760]{0:T(1024)(128)(4,1)} %bitcast.192), calls=%async_computation.7 | async-start | bytes 4194304 | tf_op jit(solution)/shard_map/while
  133.3 9.2 %slice-start.4 = ((s8[10485760]{0:T(1024)(128)(4,1)}), s8[4194304]{0:T(1024)(128)(4,1)S(1)}, s32[]{:S(2)}) async-start(s8[10485760]{0:T(1024)(128)(4,1)} %bitcast.192), calls=%async_computation.8 | async-start | bytes 8388608 | tf_op jit(solution)/shard_map/while
  133.3 9.2 %slice-start.5 = ((s8[10485760]{0:T(1024)(128)(4,1)}), s8[4194304]{0:T(1024)(128)(4,1)S(1)}, s32[]{:S(2)}) async-start(s8[10485760]{0:T(1024)(128)(4,1)} %bitcast.192), calls=%async_computation.9 | async-start | bytes 8388608 | tf_op jit(solution)/shard_map/while
  212.9 10.5 %slice-start = ((s8[10485760]{0:T(1024)(128)(4,1)}), s8[2097152]{0:T(1024)(128)(4,1)S(1)}, s32[]{:S(2)}) async-start(s8[10485760]{0:T(1024)(128)(4,1)} %bitcast.190), calls=%async_computation.4 | async-start | bytes 4194304 | tf_op jit(solution)/shard_map/while
  214.3 9.1 %slice-start.1 = ((s8[10485760]{0:T(1024)(128)(4,1)}), s8[4194304]{0:T(1024)(128)(4,1)S(1)}, s32[]{:S(2)}) async-start(s8[10485760]{0:T(1024)(128)(4,1)} %bitcast.190), calls=%async_computation.5 | async-start | bytes 8388608 | tf_op jit(solution)/shard_map/while
  214.3 9.1 %slice-start.2 = ((s8[10485760]{0:T(1024)(128)(4,1)}), s8[4194304]{0:T(1024)(128)(4,1)S(1)}, s32[]{:S(2)}) async-start(s8[10485760]{0:T(1024)(128)(4,1)} %bitcast.190), calls=%async_computation.6 | async-start | bytes 8388608 | tf_op jit(solution)/shard_map/while
  238.3 10.5 %slice-start = ((s8[10485760]{0:T(1024)(128)(4,1)}), s8[2097152]{0:T(1024)(128)(4,1)S(1)}, s32[]{:S(2)}) async-start(s8[10485760]{0:T(1024)(128)(4,1)} %bitcast.190), calls=%async_computation.4 | async-start | bytes 4194304 | tf_op jit(solution)/shard_map/while
  239.6 9.1 %slice-start.1 = ((s8[10485760]{0:T(1024)(128)(4,1)}), s8[4194304]{0:T(1024)(128)(4,1)S(1)}, s32[]{:S(2)}) async-start(s8[10485760]{0:T(1024)(128)(4,1)} %bitcast.190), calls=%async_computation.5 | async-start | bytes 8388608 | tf_op jit(solution)/shard_map/while
  239.6 9.1 %slice-start.2 = ((s8[10485760]{0:T(1024)(128)(4,1)}), s8[4194304]{0:T(1024)(128)(4,1)S(1)}, s32[]{:S(2)}) async-start(s8[10485760]{0:T(1024)(128)(4,1)} %bitcast.190), calls=%async_computation.6 | async-start | bytes 8388608 | tf_op jit(solution)/shard_map/while
Sparse Core Ops, SparseCore 0:
  42.9 23.6 all-gather.4
  77.0 23.8 all-gather.6
  103.0 49.0 all-gather.8
  154.2 47.5 all-gather.10
where the time goes:
time: 263 us
  waiting for transfers between devices  76.5 us (29%)
  blocking collectives  68.5 us (26%)
  matrix products  63.9 us (24%)
  local copies, waits for them, and re-layouts  20 us (8%)
  other arithmetic  19.6 us (7%)
  between operations  13.9 us (5%)
    all_gather x1, waiting for transfers between devices, shards(): value_rows = lax.all_gather(suffix_values, 'seq', axis=1, tiled=True)  49.6 us
    dot_general x4, matrix products, softmax_step(): jnp.einsum(form, rounded, value_rows, preferred_element_type=jnp.float32)  35.9 us
    all_gather x1, blocking collectives, shards(): lax.all_gather(own_keys, 'seq', axis=0, tiled=True)  35.3 us
    all_gather x1, blocking collectives, shards(): lax.all_gather(own_values, 'seq', axis=0, tiled=True)  33.2 us
    all_gather x1, waiting for transfers between devices, shards(): lax.all_gather(shares[1], 'samp', axis=0, tiled=True)  19.7 us
    dot_general x2, matrix products, suffix_one_step(): jnp.einsum('sqgjd,srgd->sgjqr', query_grid, key_grid, preferred_element_t...  14.5 us
    dot_general x2, matrix products, prefix_one_step(): jnp.einsum('sqgjd,rgd->sgjqr', query_grid, key_grid, preferred_element_ty...  13.5 us
    reduce_sum x4, other arithmetic, softmax_step(): new_sum = run_sum * scale_old + jnp.sum(weights, axis=-1)  9.15 us
  transfers between devices with their start and end apart: 4, of which 3 were waited for; matrix products, arithmetic and copies ran while one was open for 18% of the time, Pallas kernels for 0%

commit v1 on v0

--- a/solution.py
+++ b/solution.py
@@ -99,8 +99,13 @@
         ),
     )
     suffix_carry = carry
-    key_rows = lax.all_gather(suffix_keys, "seq", axis=1, tiled=True)
-    value_rows = lax.all_gather(suffix_values, "seq", axis=1, tiled=True)
+    key_rows, value_rows = jnp.split(
+        lax.all_gather(
+            jnp.concatenate([suffix_keys, suffix_values], axis=0), "seq", axis=1, tiled=True
+        ),
+        [suffix_keys.shape[0]],
+        axis=0,
+    )
     count = key_rows.shape[1]
     size = block_size(count)
     steps = count // size

time: 263 us -> 240 us (0.913)
  waiting for transfers between devices: 76.5 us -> 49.4 us
  local copies, waits for them, and re-layouts: 20 us -> 24.5 us
    all_gather x2 -> x1, waiting for transfers between devices: 55.5 us -> 29.3 us  [shards(): lax.all_gather(jnp.concatenate([suffix_keys, suffix_values], axis=0), 'se...]
    split x0 -> x1, local copies, waits for them, and re-layouts: none -> 4.63 us  [shards(): jnp.split(lax.all_gather(jnp.concatenate([suffix_keys, suffix_values], ax...]
  transfers between devices with their start and end apart: 4 -> 3, of which waited for: 3 -> 2; matrix products, arithmetic and copies ran while one was open for 18% -> 21% of each run, Pallas kernels for 0% -> 0%
where the time goes in v1:
time: 240 us
  blocking collectives  68.5 us (29%)
  matrix products  64 us (27%)
  waiting for transfers between devices  49.4 us (21%)
  local copies, waits for them, and re-layouts  24.5 us (10%)
  other arithmetic  19.2 us (8%)
  between operations  13.9 us (6%)
    dot_general x4, matrix products, softmax_step(): jnp.einsum(form, rounded, value_rows, preferred_element_type=jnp.float32)  36.2 us
    all_gather x1, blocking collectives, shards(): lax.all_gather(own_keys, 'seq', axis=0, tiled=True)  35.3 us
    all_gather x1, blocking collectives, shards(): lax.all_gather(own_values, 'seq', axis=0, tiled=True)  33.2 us
    all_gather x1, waiting for transfers between devices, shards(): lax.all_gather(jnp.concatenate([suffix_keys, suffix_values], axis=0), 'se...  29.3 us
    all_gather x1, waiting for transfers between devices, shards(): lax.all_gather(shares[1], 'samp', axis=0, tiled=True)  20 us
    dot_general x2, matrix products, suffix_one_step(): jnp.einsum('sqgjd,srgd->sgjqr', query_grid, key_grid, preferred_element_t...  14.5 us
    dot_general x2, matrix products, prefix_one_step(): jnp.einsum('sqgjd,rgd->sgjqr', query_grid, key_grid, preferred_element_ty...  13.3 us
    reduce_sum x4, other arithmetic, softmax_step(): new_sum = run_sum * scale_old + jnp.sum(weights, axis=-1)  9.15 us
  transfers between devices with their start and end apart: 3, of which 2 were waited for; matrix products, arithmetic and copies ran while one was open for 21% of the time, Pallas kernels for 0%

profile of v1, /device:TPU:0, one launch (start us, length us, event | category | flops | bytes accessed | tf_op | source)
XLA Modules:
  0.0 239.7 jit_solution(15917443136913775346)
XLA Ops:
  6.6 0.9 copy-done
  7.5 35.3 %all_gather.15 = bf16[256,1024]{1,0:T(8,128)(2,1)} all-gather(bf16[32,1024]{1,0:T(8,128)(2,1)S(1)} %constant_dynamic-slice_fusion.6), channel_id=1, replica_groups=mesh['seq'=8,'samp'=4] {'seq'}, dimensions={0}, use_global_device_ids=true | all-gather | bytes 589824 | tf_op jit(solution)/shard_map/all_gather | solution.py:61
  42.8 0.9 constant_dynamic-slice_fusion.5
  43.7 33.2 %all_gather.17 = bf16[256,1024]{1,0:T(8,128)(2,1)} all-gather(bf16[32,1024]{1,0:T(8,128)(2,1)S(1)} %constant_dynamic-slice_fusion.5), channel_id=1, replica_groups=mesh['seq'=8,'samp'=4] {'seq'}, dimensions={0}, use_global_device_ids=true | all-gather | bytes 589824 | tf_op jit(solution)/shard_map/all_gather | solution.py:62
  77.0 0.9 pad_maximum_fusion
  77.9 0.8 copy.39
  78.7 1.4 copy.41
  80.9 20.0 %all-gather.6.cloned.1.call-done = bf16[1024,1024]{1,0:T(8,128)(2,1)} async-done(((bf16[256,1024]{1,0:T(8,128)(2,1)}), bf16[1024,1024]{1,0:T(8,128)(2,1)}) %all-gather.6.cloned.1.call-update) | async-done | bytes 2097168 | tf_op jit(solution)/shard_map/all_gather | solution.py:66
  100.9 45.7 %while.35 = (s32[]{:T(128)}, f32[1,8,5,128]{3,2,1,0:T(8,128)S(1)}, f32[1,8,5,128]{3,2,1,0:T(8,128)}, f32[1,128,8,5,128]{1,4,3,2,0:T(8,128)}, s32[2,512]{1,0:T(2,...) while((s32[]{:T(128)}, f32[1,8,5,128]{3,2,1,0:T(8,128)S(1)}, ...), condition=%wide.region_4.5_spmd.clone, body=%wide.region_0.4_spmd.clone.sunk | while | flops 1373029888 | bytes 80294112 | solution.py:92
  100.9 0.1 select_reduce_fusion.5
  101.0 1.7 constant_dynamic-slice_fusion.11
  102.7 0.5 copy.67
  103.3 6.7 %fusion.67 = (f32[8,5,128]{2,1,0:T(8,128)S(1)}, f32[8,512,128,5]{2,1,3,0:T(8,128)}) fusion(pred[512]{0:T(512)(128)(4,1)S(1)} %broadcast_compare_fusion.5, bf16[512,8,128,1]{0,2,3,1:T(8,128)(2,1)S(1)} %bitcast.194, bf16[1,128,8,5,128]{4,1,3,2,0:T(8,128)(2,1)} %get-tuple-element.615), kind=kOutput, calls=%fused_computation.3.clone.1 | convolution fusion | flops 678947840 | bytes 12866048 | tf_op jit(solution)/shard_map/while/body/eval_jaxpr/sqgjd,rgd->sgjqr/dot_general | solution.py:84
  110.0 1.4 copy.68
  111.4 8.5 %bitcast_add_fusion.11 = f32[1,128,8,5,128]{1,4,3,2,0:T(8,128)} fusion(f32[1,128,8,5,128]{1,4,3,2,0:T(8,128)} %get-tuple-element.600, bf16[512,8,128,1]{0,2,3,1:T(8,128)(2,1)} %bitcast.197, f32[8,512,128,5]{2,1,3,0:T(8,128)} %get-tuple-element.583, f32[8,5,128]{2,1,0:T(8,128)S(1)} %bitcast.202, pred[512]{0:T(512)(128)(4,1)S(1)} %broadcast_compare_fusion.5, ...), kind=kOutput, calls=%fused_computation.14.clone.1 | convolution fusion | flops 683540480 | bytes 16818688 | tf_op jit(solution)/shard_map/while/body/eval_jaxpr/sgjqr,rgd->sqgjd/dot_general | solution.py:27
  119.9 2.3 fusion.69
  122.2 0.6 bitcast_add_fusion.10
  122.8 0.1 select_reduce_fusion.5
  122.9 1.7 constant_dynamic-slice_fusion.11
  124.7 0.5 copy.67
  125.2 6.6 %fusion.67 = (f32[8,5,128]{2,1,0:T(8,128)S(1)}, f32[8,512,128,5]{2,1,3,0:T(8,128)}) fusion(pred[512]{0:T(512)(128)(4,1)S(1)} %broadcast_compare_fusion.5, bf16[512,8,128,1]{0,2,3,1:T(8,128)(2,1)S(1)} %bitcast.194, bf16[1,128,8,5,128]{4,1,3,2,0:T(8,128)(2,1)} %get-tuple-element.615), kind=kOutput, calls=%fused_computation.3.clone.1 | convolution fusion | flops 678947840 | bytes 12866048 | tf_op jit(solution)/shard_map/while/body/eval_jaxpr/sqgjd,rgd->sgjqr/dot_general | solution.py:84
  131.9 1.4 copy.68
  133.3 9.6 %bitcast_add_fusion.11 = f32[1,128,8,5,128]{1,4,3,2,0:T(8,128)} fusion(f32[1,128,8,5,128]{1,4,3,2,0:T(8,128)} %get-tuple-element.600, bf16[512,8,128,1]{0,2,3,1:T(8,128)(2,1)} %bitcast.197, f32[8,512,128,5]{2,1,3,0:T(8,128)} %get-tuple-element.583, f32[8,5,128]{2,1,0:T(8,128)S(1)} %bitcast.202, pred[512]{0:T(512)(128)(4,1)S(1)} %broadcast_compare_fusion.5, ...), kind=kOutput, calls=%fused_computation.14.clone.1 | convolution fusion | flops 683540480 | bytes 16818688 | tf_op jit(solution)/shard_map/while/body/eval_jaxpr/sgjqr,rgd->sqgjd/dot_general | solution.py:27
  142.9 2.3 fusion.69
  145.2 1.4 bitcast_add_fusion.10
  146.6 29.3 %all-gather.8.cloned.1.call-done = bf16[2,1024,1024]{2,1,0:T(8,128)(2,1)} async-done(((bf16[2,128,1024]{2,1,0:T(8,128)(2,1)}), bf16[2,1024,1024]{2,1,0:T(8,128)(2,1)}) %all-gather.8.cloned.1.call-update) | async-done | bytes 4194320 | tf_op jit(solution)/shard_map/all_gather | solution.py:103
  175.9 4.6 %fusion.41 = (bf16[1,1024,1024]{2,1,0:T(8,128)(2,1)}, bf16[1,1024,1024]{2,1,0:T(8,128)(2,1)}) fusion(bf16[2,1024,1024]{2,1,0:T(8,128)(2,1)} %all-gather.8.cloned.1.call-done), kind=kLoop, calls=%fused_computation.85 | loop fusion | bytes 8388608 | tf_op jit(solution)/shard_map/split | solution.py:102
  180.6 49.1 %while.34 = (s32[]{:T(128)}, f32[1,8,5,128]{3,2,1,0:T(8,128)S(1)}, f32[1,8,5,128]{3,2,1,0:T(8,128)}, f32[1,128,8,5,128]{1,4,3,2,0:T(8,128)}, s32[2,512]{1,0:T(2,...) while((s32[]{:T(128)}, f32[1,8,5,128]{3,2,1,0:T(8,128)S(1)}, ...), condition=%wide.region_9.10_spmd.clone, body=%wide.region_5.9_spmd.clone.sunk | while | flops 1372491392 | bytes 80563432 | solution.py:133
  180.7 0.2 compare_and_fusion.2
  180.9 1.7 constant_dynamic-slice_fusion.10
  182.6 0.5 copy.65
  183.2 7.2 %fusion.61 = (f32[8,5,128]{2,1,0:T(8,128)S(1)}, f32[8,512,128,5]{2,1,3,0:T(8,128)}) fusion(pred[128,512]{0,1:T(8,128)(4,1)S(1)} %compare_and_fusion.2, bf16[512,8,128,1]{0,2,3,1:T(8,128)(2,1)S(1)} %bitcast.195, bf16[1,128,8,5,128]{4,1,3,2,0:T(8,128)(2,1)} %get-tuple-element.651), kind=kOutput, calls=%fused_computation.36.clone.1 | convolution fusion | flops 678947840 | bytes 12931072 | tf_op jit(solution)/shard_map/while/body/eval_jaxpr/sqgjd,srgd->sgjqr/dot_general | solution.py:120
  190.4 0.6 fusion.62
  191.0 1.3 copy.66
  192.4 9.0 %bitcast_add_fusion.9 = f32[1,128,8,5,128]{1,4,3,2,0:T(8,128)} fusion(f32[1,128,8,5,128]{1,4,3,2,0:T(8,128)} %get-tuple-element.634, bf16[512,8,128,1]{0,2,3,1:T(8,128)(2,1)} %bitcast.196, f32[8,512,128,5]{2,1,3,0:T(8,128)} %get-tuple-element.568, f32[8,5,128]{2,1,0:T(8,128)S(1)} %bitcast.200, pred[128,512]{0,1:T(8,128)(4,1)S(1)} %compare_and_fusion.2, ...), kind=kOutput, calls=%fused_computation.47.clone.1 | convolution fusion | flops 682885120 | bytes 16883712 | tf_op jit(solution)/shard_map/while/body/eval_jaxpr/sgjqr,srgd->sqgjd/dot_general | solution.py:27
  201.4 2.3 fusion.63
  203.7 1.4 bitcast_add_fusion.8
  205.2 0.2 compare_and_fusion.2
  205.4 1.7 constant_dynamic-slice_fusion.10
  207.2 0.5 copy.65
  207.7 7.2 %fusion.61 = (f32[8,5,128]{2,1,0:T(8,128)S(1)}, f32[8,512,128,5]{2,1,3,0:T(8,128)}) fusion(pred[128,512]{0,1:T(8,128)(4,1)S(1)} %compare_and_fusion.2, bf16[512,8,128,1]{0,2,3,1:T(8,128)(2,1)S(1)} %bitcast.195, bf16[1,128,8,5,128]{4,1,3,2,0:T(8,128)(2,1)} %get-tuple-element.651), kind=kOutput, calls=%fused_computation.36.clone.1 | convolution fusion | flops 678947840 | bytes 12931072 | tf_op jit(solution)/shard_map/while/body/eval_jaxpr/sqgjd,srgd->sgjqr/dot_general | solution.py:120
  214.9 0.6 fusion.62
  215.6 1.3 copy.66
  216.9 9.0 %bitcast_add_fusion.9 = f32[1,128,8,5,128]{1,4,3,2,0:T(8,128)} fusion(f32[1,128,8,5,128]{1,4,3,2,0:T(8,128)} %get-tuple-element.634, bf16[512,8,128,1]{0,2,3,1:T(8,128)(2,1)} %bitcast.196, f32[8,512,128,5]{2,1,3,0:T(8,128)} %get-tuple-element.568, f32[8,5,128]{2,1,0:T(8,128)S(1)} %bitcast.200, pred[128,512]{0,1:T(8,128)(4,1)S(1)} %compare_and_fusion.2, ...), kind=kOutput, calls=%fused_computation.47.clone.1 | convolution fusion | flops 682885120 | bytes 16883712 | tf_op jit(solution)/shard_map/while/body/eval_jaxpr/sgjqr,srgd->sqgjd/dot_general | solution.py:27
  225.9 2.3 fusion.63
  228.2 1.4 bitcast_add_fusion.8
  229.6 2.1 select_convert_fusion
  231.7 1.4 copy.46
  (72 shorter events, 0.7 us)
Async XLA Ops:
  6.5 1.0 copy-start
  6.5 70.4 %copy-start.3 = (bf16[1,128,1024]{2,1,0:T(8,128)(2,1)S(1)}, bf16[1,128,1024]{2,1,0:T(8,128)(2,1)}, u32[]{:S(2)}) copy-start(bf16[1,128,1024]{2,1,0:T(8,128)(2,1)} %param.15) | copy-start | bytes 786436
  6.5 70.4 %copy-start.2 = (bf16[1,128,1024]{2,1,0:T(8,128)(2,1)S(1)}, bf16[1,128,1024]{2,1,0:T(8,128)(2,1)}, u32[]{:S(2)}) copy-start(bf16[1,128,1024]{2,1,0:T(8,128)(2,1)} %param.16) | copy-start | bytes 786436
  6.5 71.3 %copy-start.1 = (bf16[1,128,5120]{2,1,0:T(8,128)(2,1)S(1)}, bf16[1,128,5120]{2,1,0:T(8,128)(2,1)}, u32[]{:S(2)}) copy-start(bf16[1,128,5120]{2,1,0:T(8,128)(2,1)} %param.12) | copy-start | bytes 3932164
  6.5 74.3 %all-gather.4.cloned.1.call-start = ((), (), s32[]{:S(2)}) async-start(), calls=%async_computation | async-start | bytes 2621440 | tf_op jit(solution)/shard_map/all_gather | solution.py:65
  42.8 58.1 %all-gather.6.cloned.1.call-start = ((), (), s32[]{:S(2)}) async-start(), calls=%async_computation.1 | async-start | bytes 2621440 | tf_op jit(solution)/shard_map/all_gather | solution.py:66
  76.9 99.0 %all-gather.8.cloned.1.call-start = ((), (), s32[]{:S(2)}) async-start(), calls=%async_computation.2 | async-start | bytes 4718592 | tf_op jit(solution)/shard_map/all_gather | solution.py:103
  77.9 23.0 %copy-start.4 = (s32[1,1,8]{2,1,0:T(1,128)S(1)}, s32[1,1,8]{2,1,0:T(1,128)}, u32[]{:S(2)}) copy-start(s32[1,1,8]{2,1,0:T(1,128)} %param.17) | copy-start | bytes 100
  110.0 9.9 %slice-start.3 = ((s8[10485760]{0:T(1024)(128)(4,1)}), s8[2097152]{0:T(1024)(128)(4,1)S(1)}, s32[]{:S(2)}) async-start(s8[10485760]{0:T(1024)(128)(4,1)} %bitcast.192), calls=%async_computation.6 | async-start | bytes 4194304 | tf_op jit(solution)/shard_map/while
  111.4 8.5 %slice-start.4 = ((s8[10485760]{0:T(1024)(128)(4,1)}), s8[4194304]{0:T(1024)(128)(4,1)S(1)}, s32[]{:S(2)}) async-start(s8[10485760]{0:T(1024)(128)(4,1)} %bitcast.192), calls=%async_computation.7 | async-start | bytes 8388608 | tf_op jit(solution)/shard_map/while
  111.4 8.5 %slice-start.5 = ((s8[10485760]{0:T(1024)(128)(4,1)}), s8[4194304]{0:T(1024)(128)(4,1)S(1)}, s32[]{:S(2)}) async-start(s8[10485760]{0:T(1024)(128)(4,1)} %bitcast.192), calls=%async_computation.8 | async-start | bytes 8388608 | tf_op jit(solution)/shard_map/while
  131.9 11.0 %slice-start.3 = ((s8[10485760]{0:T(1024)(128)(4,1)}), s8[2097152]{0:T(1024)(128)(4,1)S(1)}, s32[]{:S(2)}) async-start(s8[10485760]{0:T(1024)(128)(4,1)} %bitcast.192), calls=%async_computation.6 | async-start | bytes 4194304 | tf_op jit(solution)/shard_map/while
  133.3 9.6 %slice-start.4 = ((s8[10485760]{0:T(1024)(128)(4,1)}), s8[4194304]{0:T(1024)(128)(4,1)S(1)}, s32[]{:S(2)}) async-start(s8[10485760]{0:T(1024)(128)(4,1)} %bitcast.192), calls=%async_computation.7 | async-start | bytes 8388608 | tf_op jit(solution)/shard_map/while
  133.3 9.6 %slice-start.5 = ((s8[10485760]{0:T(1024)(128)(4,1)}), s8[4194304]{0:T(1024)(128)(4,1)S(1)}, s32[]{:S(2)}) async-start(s8[10485760]{0:T(1024)(128)(4,1)} %bitcast.192), calls=%async_computation.8 | async-start | bytes 8388608 | tf_op jit(solution)/shard_map/while
  146.6 34.0 %copy-start.5 = (s32[1,1,8]{2,1,0:T(1,128)S(1)}, s32[1,1,8]{2,1,0:T(1,128)}, u32[]{:S(2)}) copy-start(s32[1,1,8]{2,1,0:T(1,128)} %param.18) | copy-start | bytes 100
  191.0 10.3 %slice-start = ((s8[10485760]{0:T(1024)(128)(4,1)}), s8[2097152]{0:T(1024)(128)(4,1)S(1)}, s32[]{:S(2)}) async-start(s8[10485760]{0:T(1024)(128)(4,1)} %bitcast.190), calls=%async_computation.3 | async-start | bytes 4194304 | tf_op jit(solution)/shard_map/while
  192.4 9.0 %slice-start.1 = ((s8[10485760]{0:T(1024)(128)(4,1)}), s8[4194304]{0:T(1024)(128)(4,1)S(1)}, s32[]{:S(2)}) async-start(s8[10485760]{0:T(1024)(128)(4,1)} %bitcast.190), calls=%async_computation.4 | async-start | bytes 8388608 | tf_op jit(solution)/shard_map/while
  192.4 9.0 %slice-start.2 = ((s8[10485760]{0:T(1024)(128)(4,1)}), s8[4194304]{0:T(1024)(128)(4,1)S(1)}, s32[]{:S(2)}) async-start(s8[10485760]{0:T(1024)(128)(4,1)} %bitcast.190), calls=%async_computation.5 | async-start | bytes 8388608 | tf_op jit(solution)/shard_map/while
  215.6 10.4 %slice-start = ((s8[10485760]{0:T(1024)(128)(4,1)}), s8[2097152]{0:T(1024)(128)(4,1)S(1)}, s32[]{:S(2)}) async-start(s8[10485760]{0:T(1024)(128)(4,1)} %bitcast.190), calls=%async_computation.3 | async-start | bytes 4194304 | tf_op jit(solution)/shard_map/while
  216.9 9.0 %slice-start.1 = ((s8[10485760]{0:T(1024)(128)(4,1)}), s8[4194304]{0:T(1024)(128)(4,1)S(1)}, s32[]{:S(2)}) async-start(s8[10485760]{0:T(1024)(128)(4,1)} %bitcast.190), calls=%async_computation.4 | async-start | bytes 8388608 | tf_op jit(solution)/shard_map/while
  216.9 9.0 %slice-start.2 = ((s8[10485760]{0:T(1024)(128)(4,1)}), s8[4194304]{0:T(1024)(128)(4,1)S(1)}, s32[]{:S(2)}) async-start(s8[10485760]{0:T(1024)(128)(4,1)} %bitcast.190), calls=%async_computation.5 | async-start | bytes 8388608 | tf_op jit(solution)/shard_map/while
Sparse Core Ops, SparseCore 0:
  42.9 23.6 all-gather.3
  77.0 23.8 all-gather.5
  103.1 72.7 all-gather.7
